TPU v7x, 32 devices: a whole 2x2x4 slice. The times are simulated.
32 devices in a mesh: tm: 8 (over y, x, core), chan: 4 (over z).
Axes of the slice: x: 2, y: 2, z: 4, core: 2. Of those that a mesh axis runs over, the one named last changes fastest.
Arguments:
- samples: bfloat16 [2, 16384, 2048], P(None, ('tm', 'chan')), may hold values from -6 to 6
- taps: float32 [8, 2048], replicated, may hold values from -2.5 to 2.5
Outputs:
- spectra: bfloat16 [2, 2, 1024, 16384], P(None, None, ('tm', 'chan'))
All inputs are finite; a program needn't handle non-finite values.
Results may differ from a plain program's by a relative error of at most 0.0055.
Values may be sent and summed in bfloat16 or wider, within the bound.
A program may use at most 64 MiB of HBM per device.

v0:
```python
import functools

import jax
import jax.numpy as jnp
import numpy as np
from jax import lax
from jax.experimental import pallas as pl
from jax.experimental.pallas import tpu as pltpu
from jax.sharding import PartitionSpec as P

MESH = pl.DeviceIdType.MESH
HALO = 16
ROWS = 128
LANES = 128


def base_tables(nfft, per_dev, count):
    n = np.arange(nfft, dtype=np.int64)[None, :]

    def pair(steps, scale):
        angle = (steps[:, None] * n % nfft) * (2.0 * np.pi / nfft)
        return np.stack([np.cos(angle) * scale, np.sin(angle) * scale]).astype(np.float32)

    coarse = pair(np.arange(count, dtype=np.int64) * per_dev, 1.0 / 32.0)
    fine = pair(np.arange(per_dev, dtype=np.int64), 1.0)
    return coarse, fine


def kernel(
    tms, chans, samples, taps, coarse, fine, out,
    xs, weighted, table, sp, load_sem, halo_sem, own_sem, send_sem, recv_sem,
):
    pols, frames, nfft = samples.shape
    tap_count = taps.shape[0]
    per_dev = fine.shape[1]
    count = tms * chans
    half = frames // 2
    my_tm, my_z = lax.axis_index("tm"), lax.axis_index("chan")
    me = my_tm * chans + my_z

    loads = [
        pltpu.make_async_copy(
            samples.at[p, pl.ds(low, size)], xs.at[p, pl.ds(HALO + low, size)], load_sem.at[at, p]
        )
        for at, (low, size) in enumerate([(half - HALO, half + HALO), (0, half - HALO)])
        for p in range(pols)
    ]
    for load in loads:
        load.start()

    barrier = pltpu.get_barrier_semaphore()

    def greet(step, _):
        peer = lax.rem(me + step, count)
        pl.semaphore_signal(
            barrier, inc=1, device_id=(peer // chans, lax.rem(peer, chans)), device_id_type=MESH
        )
        return 0

    lax.fori_loop(1, count, greet, 0)

    after = lax.rem(me + 1, count)
    halo = pltpu.make_async_remote_copy(
        src_ref=samples.at[:, pl.ds(frames - HALO, HALO), :],
        dst_ref=xs.at[:, pl.ds(0, HALO), :],
        send_sem=halo_sem.at[0],
        recv_sem=halo_sem.at[1],
        device_id=(after // chans, lax.rem(after, chans)),
        device_id_type=MESH,
    )

    def filter_chunk(p, low, size):
        blocks = size // ROWS
        lane_blocks = nfft // LANES

        def body(step, _):
            row = pl.multiple_of((step // lane_blocks) * ROWS, ROWS)
            lane = pl.multiple_of(lax.rem(step, lane_blocks) * LANES, LANES)
            x = xs[p, pl.ds(low + row, ROWS + HALO), pl.ds(lane, LANES)]
            x = x.astype(jnp.float32)
            w = taps[:, pl.ds(lane, LANES)]
            total = None
            for tap in range(tap_count):
                by = tap_count - 1 - tap
                moved = x if by == 0 else pltpu.roll(x, by, 0)
                term = w[tap : tap + 1, :] * moved[HALO:, :]
                total = term if total is None else total + term
            weighted[pl.ds(row, ROWS), pl.ds(lane, LANES)] = total.astype(jnp.bfloat16)
            return 0

        lax.fori_loop(0, blocks * lane_blocks, body, 0)

    def make_group(z):
        def body(tm, _):
            dest = tm * chans + z
            cos_i, sin_i = coarse[0, pl.ds(dest, 1), :], coarse[1, pl.ds(dest, 1), :]
            cos_j, sin_j = fine[0], fine[1]
            table[z, tm, 0] = (cos_i * cos_j - sin_i * sin_j).astype(jnp.bfloat16)
            table[z, tm, 1] = (-(sin_i * cos_j + cos_i * sin_j)).astype(jnp.bfloat16)
            return 0

        lax.fori_loop(0, tms, body, 0)

    def group_of(step):
        return lax.bitwise_xor(my_z, lax.bitwise_xor(step, chans // 2))

    make_group(group_of(jnp.int32(0)))

    def chunk(p, low, size, first):
        def group(step, _):
            z = group_of(step)
            rows = table[z].reshape(tms * 2 * per_dev, nfft)
            product = lax.dot_general(
                rows, weighted[pl.ds(0, size), :], (((1,), (1,)), ((), ())),
                preferred_element_type=jnp.float32,
            )
            product = product.reshape(tms, 2, per_dev, size)
            sp[z, :, :, p, :, low : low + size] = product.astype(jnp.bfloat16)
            if first:
                @pl.when(step == 0)
                def _():
                    pl.semaphore_wait(barrier, count - 1)
                    halo.start()

            def send(turn_by, _):
                tm = lax.rem(my_tm + turn_by, tms)
                dest = tm * chans + z

                @pl.when(dest != me)
                def _():
                    pltpu.make_async_remote_copy(
                        src_ref=sp.at[z, tm, :, p, :, pl.ds(low, size)],
                        dst_ref=out.at[:, p, :, pl.ds(pl.multiple_of(me * frames + low, LANES), size)],
                        send_sem=send_sem.at[dest],
                        recv_sem=recv_sem.at[me],
                        device_id=(tm, z),
                        device_id_type=MESH,
                    ).start()

                return 0

            lax.fori_loop(0, tms, send, 0)
            if first:
                @pl.when(step < chans - 1)
                def _():
                    make_group(group_of(step + 1))

            return 0

        filter_chunk(p, low, size)
        lax.fori_loop(0, chans, group, 0)

    quarter = frames // 4
    loads[0].wait()
    chunk(0, frames - quarter, quarter, True)
    chunk(0, half, quarter, False)
    for p in range(1, pols):
        loads[p].wait()
        chunk(p, half, half, False)
    halo.wait()

    @pl.when(me == 0)
    def _():
        xs[:, 0:HALO, :] = jnp.zeros((pols, HALO, nfft), jnp.bfloat16)

    for p in range(pols):
        loads[pols + p].wait()
        chunk(p, 0, half, False)

    own = pltpu.make_async_copy(
        sp.at[my_z, my_tm],
        out.at[:, :, :, pl.ds(pl.multiple_of(me * frames, frames), frames)],
        own_sem,
    )
    own.start()

    def finish(step, _):
        peer = lax.rem(me + step, count)
        pltpu.make_async_remote_copy(
            src_ref=sp.at[lax.rem(peer, chans), peer // chans],
            dst_ref=out.at[:, :, :, pl.ds(pl.multiple_of(peer * frames, frames), frames)],
            send_sem=send_sem.at[peer],
            recv_sem=recv_sem.at[peer],
            device_id=(peer // chans, lax.rem(peer, chans)),
            device_id_type=MESH,
        ).wait()
        return 0

    lax.fori_loop(1, count, finish, 0)
    own.wait()


def local(tms, chans, samples, taps):
    pols, frames, nfft = samples.shape
    count = tms * chans
    per_dev = nfft // 2 // count
    coarse, fine = base_tables(nfft, per_dev, count)
    vmem = pl.BlockSpec(memory_space=pltpu.VMEM)
    hbm = pl.BlockSpec(memory_space=pl.ANY)
    return pl.pallas_call(
        functools.partial(kernel, tms, chans),
        out_shape=pltpu.VMEM((2, pols, per_dev, frames * count), jnp.bfloat16),
        in_specs=[hbm, vmem, vmem, vmem],
        out_specs=vmem,
        scratch_shapes=[
            pltpu.VMEM((pols, HALO + frames, nfft), jnp.bfloat16),
            pltpu.VMEM((frames // 2, nfft), jnp.bfloat16),
            pltpu.VMEM((chans, tms, 2, per_dev, nfft), jnp.bfloat16),
            pltpu.VMEM((chans, tms, 2, pols, per_dev, frames), jnp.bfloat16),
            pltpu.SemaphoreType.DMA((2, pols)),
            pltpu.SemaphoreType.DMA((2,)),
            pltpu.SemaphoreType.DMA,
            pltpu.SemaphoreType.DMA((count,)),
            pltpu.SemaphoreType.DMA((count,)),
        ],
        compiler_params=pltpu.CompilerParams(
            collective_id=0, has_side_effects=True, vmem_limit_bytes=56 * 1024 * 1024
        ),
    )(samples, taps, jnp.asarray(coarse), jnp.asarray(fine))


def solution(mesh):
    return jax.shard_map(
        functools.partial(local, mesh.shape["tm"], mesh.shape["chan"]),
        mesh=mesh,
        in_specs=(P(None, ("tm", "chan"), None), P()),
        out_specs=P(None, None, ("tm", "chan"), None),
        check_vma=False,
    )
```

profile of v0, /device:TPU:13, one launch (start us, length us, event | category | flops | bytes accessed | tf_op | source)
XLA Modules:
  0.0 103.4 jit_solution(13374027539361222964)
XLA Ops:
  0.0 101.4 %shard_map.46 = bf16[2,2,32,16384]{3,2,1,0:T(8,128)(2,1)S(1)} custom-call(bf16[2,512,2048]{2,1,0:T(8,128)(2,1)} %samples.1, f32[8,2048]{1,0:T(8,128)} %taps.1, f32[2,32,2048]{2,1,0:T(8,128)} %constant.4.clone.coarse, f32[2,32,2048]{2,1,0:T(8,128)} %constant.5.clone.fine), custom_call_target="tpu_custom_call" | custom-call | tf_op jit(solution)/shard_map/pallas_call | solution.py:200
  101.4 2.0 %copy.6 = bf16[2,2,32,16384]{3,2,1,0:T(8,128)(2,1)} copy(bf16[2,2,32,16384]{3,2,1,0:T(8,128)(2,1)S(1)} %shard_map.46) | data formatting | bytes 8388608
where the time goes:
time: 104 us; the launch traced here: 103 us
  Pallas kernels  101 us (97%)
  local copies, waits for them, and re-layouts  2.02 us (2%)
    pallas_call x1, Pallas kernels, local(): pl.pallas_call(functools.partial(kernel, tms, chans), out_shape=pltpu.VME...  101 us

commit v1 on v0

--- a/solution.py
+++ b/solution.py
@@ -9,7 +9,7 @@
 from jax.sharding import PartitionSpec as P
 
 MESH = pl.DeviceIdType.MESH
-HALO = 16
+HALO = 8
 ROWS = 128
 LANES = 128
 
@@ -27,37 +27,58 @@
 
 
 def kernel(
-    tms, chans, samples, taps, coarse, fine, out,
-    xs, weighted, table, sp, load_sem, halo_sem, own_sem, send_sem, recv_sem,
+    tms, chans, samples, taps_in, coarse_in, fine_in, out,
+    xs, taps, coarse, fine, weighted, table, sp,
+    load_sem, base_sem, coarse_sem, halo_sem, own_sem, send_sem, recv_sem,
 ):
     pols, frames, nfft = samples.shape
-    tap_count = taps.shape[0]
-    per_dev = fine.shape[1]
+    tap_count = taps_in.shape[0]
+    per_dev = fine_in.shape[1]
     count = tms * chans
     half = frames // 2
+    quarter = frames // 4
     my_tm, my_z = lax.axis_index("tm"), lax.axis_index("chan")
     me = my_tm * chans + my_z
 
+    def group_of(step):
+        return lax.bitwise_xor(my_z, lax.bitwise_xor(step, chans // 2))
+
+    def coarse_load(step):
+        z = group_of(step)
+        return pltpu.make_async_copy(coarse_in.at[z], coarse.at[z], coarse_sem.at[step])
+
+    taps_load = pltpu.make_async_copy(taps_in, taps, base_sem.at[0])
+    fine_load = pltpu.make_async_copy(fine_in, fine, base_sem.at[1])
+    spans = [
+        (0, frames - quarter - HALO, quarter + HALO),
+        (0, half - HALO, quarter),
+        *((p, half - HALO, half + HALO) for p in range(1, pols)),
+        *((p, 0, half - HALO) for p in range(pols)),
+    ]
     loads = [
         pltpu.make_async_copy(
-            samples.at[p, pl.ds(low, size)], xs.at[p, pl.ds(HALO + low, size)], load_sem.at[at, p]
+            samples.at[p, pl.ds(low, size)], xs.at[p, pl.ds(HALO + low, size)], load_sem.at[at]
         )
-        for at, (low, size) in enumerate([(half - HALO, half + HALO), (0, half - HALO)])
-        for p in range(pols)
+        for at, (p, low, size) in enumerate(spans)
     ]
-    for load in loads:
+    fine_load.start()
+    coarse_load(0).start()
+    taps_load.start()
+    loads[0].start()
+
+    barrier = pltpu.get_barrier_semaphore()
+
+    for step in range(chans):
+        for turn_by in range(tms):
+            z, tm = group_of(step), lax.rem(my_tm + turn_by, tms)
+
+            if (step, turn_by) != (chans // 2, 0):
+                pl.semaphore_signal(barrier, inc=1, device_id=(tm, z), device_id_type=MESH)
+
+    for step in range(1, chans):
+        coarse_load(step).start()
+    for load in loads[1:]:
         load.start()
-
-    barrier = pltpu.get_barrier_semaphore()
-
-    def greet(step, _):
-        peer = lax.rem(me + step, count)
-        pl.semaphore_signal(
-            barrier, inc=1, device_id=(peer // chans, lax.rem(peer, chans)), device_id_type=MESH
-        )
-        return 0
-
-    lax.fori_loop(1, count, greet, 0)
 
     after = lax.rem(me + 1, count)
     halo = pltpu.make_async_remote_copy(
@@ -92,8 +113,7 @@
 
     def make_group(z):
         def body(tm, _):
-            dest = tm * chans + z
-            cos_i, sin_i = coarse[0, pl.ds(dest, 1), :], coarse[1, pl.ds(dest, 1), :]
+            cos_i, sin_i = coarse[z, 0, pl.ds(tm, 1), :], coarse[z, 1, pl.ds(tm, 1), :]
             cos_j, sin_j = fine[0], fine[1]
             table[z, tm, 0] = (cos_i * cos_j - sin_i * sin_j).astype(jnp.bfloat16)
             table[z, tm, 1] = (-(sin_i * cos_j + cos_i * sin_j)).astype(jnp.bfloat16)
@@ -101,9 +121,8 @@
 
         lax.fori_loop(0, tms, body, 0)
 
-    def group_of(step):
-        return lax.bitwise_xor(my_z, lax.bitwise_xor(step, chans // 2))
-
+    fine_load.wait()
+    coarse_load(0).wait()
     make_group(group_of(jnp.int32(0)))
 
     def chunk(p, low, size, first):
@@ -116,12 +135,6 @@
             )
             product = product.reshape(tms, 2, per_dev, size)
             sp[z, :, :, p, :, low : low + size] = product.astype(jnp.bfloat16)
-            if first:
-                @pl.when(step == 0)
-                def _():
-                    pl.semaphore_wait(barrier, count - 1)
-                    halo.start()
-
             def send(turn_by, _):
                 tm = lax.rem(my_tm + turn_by, tms)
                 dest = tm * chans + z
@@ -143,19 +156,24 @@
             if first:
                 @pl.when(step < chans - 1)
                 def _():
+                    coarse_load(step + 1).wait()
                     make_group(group_of(step + 1))
 
             return 0
 
         filter_chunk(p, low, size)
+        if first:
+            pl.semaphore_wait(barrier, count - 1)
+            halo.start()
         lax.fori_loop(0, chans, group, 0)
 
-    quarter = frames // 4
+    taps_load.wait()
     loads[0].wait()
     chunk(0, frames - quarter, quarter, True)
+    loads[1].wait()
     chunk(0, half, quarter, False)
     for p in range(1, pols):
-        loads[p].wait()
+        loads[1 + p].wait()
         chunk(p, half, half, False)
     halo.wait()
 
@@ -164,7 +182,7 @@
         xs[:, 0:HALO, :] = jnp.zeros((pols, HALO, nfft), jnp.bfloat16)
 
     for p in range(pols):
-        loads[pols + p].wait()
+        loads[1 + pols + p].wait()
         chunk(p, 0, half, False)
 
     own = pltpu.make_async_copy(
@@ -174,40 +192,56 @@
     )
     own.start()
 
-    def finish(step, _):
-        peer = lax.rem(me + step, count)
-        pltpu.make_async_remote_copy(
-            src_ref=sp.at[lax.rem(peer, chans), peer // chans],
+    def block(z, tm):
+        peer = tm * chans + z
+        return pltpu.make_async_remote_copy(
+            src_ref=sp.at[z, tm],
             dst_ref=out.at[:, :, :, pl.ds(pl.multiple_of(peer * frames, frames), frames)],
             send_sem=send_sem.at[peer],
             recv_sem=recv_sem.at[peer],
-            device_id=(peer // chans, lax.rem(peer, chans)),
+            device_id=(tm, z),
             device_id_type=MESH,
-        ).wait()
-        return 0
-
-    lax.fori_loop(1, count, finish, 0)
+        )
+
+    def finish_group(step):
+        z = group_of(step)
+
+        def body(turn_by, _):
+            block(z, lax.rem(my_tm + turn_by, tms)).wait()
+            return 0
+
+        lax.fori_loop(1 if step == chans // 2 else 0, tms, body, 0)
+
     own.wait()
+    for step in reversed(range(chans)):
+        finish_group(step)
 
 
 def local(tms, chans, samples, taps):
     pols, frames, nfft = samples.shape
+    tap_count = taps.shape[0]
     count = tms * chans
     per_dev = nfft // 2 // count
     coarse, fine = base_tables(nfft, per_dev, count)
+    coarse = coarse.reshape(2, tms, chans, nfft).transpose(2, 0, 1, 3)
     vmem = pl.BlockSpec(memory_space=pltpu.VMEM)
     hbm = pl.BlockSpec(memory_space=pl.ANY)
     return pl.pallas_call(
         functools.partial(kernel, tms, chans),
         out_shape=pltpu.VMEM((2, pols, per_dev, frames * count), jnp.bfloat16),
-        in_specs=[hbm, vmem, vmem, vmem],
+        in_specs=[hbm, hbm, hbm, hbm],
         out_specs=vmem,
         scratch_shapes=[
             pltpu.VMEM((pols, HALO + frames, nfft), jnp.bfloat16),
+            pltpu.VMEM((tap_count, nfft), jnp.float32),
+            pltpu.VMEM((chans, 2, tms, nfft), jnp.float32),
+            pltpu.VMEM((2, per_dev, nfft), jnp.float32),
             pltpu.VMEM((frames // 2, nfft), jnp.bfloat16),
             pltpu.VMEM((chans, tms, 2, per_dev, nfft), jnp.bfloat16),
             pltpu.VMEM((chans, tms, 2, pols, per_dev, frames), jnp.bfloat16),
-            pltpu.SemaphoreType.DMA((2, pols)),
+            pltpu.SemaphoreType.DMA((2 * pols + 1,)),
+            pltpu.SemaphoreType.DMA((2,)),
+            pltpu.SemaphoreType.DMA((chans,)),
             pltpu.SemaphoreType.DMA((2,)),
             pltpu.SemaphoreType.DMA,
             pltpu.SemaphoreType.DMA((count,)),

time: 104 us -> 101 us (0.971)
  Pallas kernels: 101 us -> 99.3 us
    pallas_call x1, Pallas kernels: 101 us -> 99.3 us  [local(): pl.pallas_call(functools.partial(kernel, tms, chans), out_shape=pltpu.VME...]
where the time goes in v1:
time: 101 us
  Pallas kernels  99.3 us (98%)
  local copies, waits for them, and re-layouts  2.02 us (2%)
    pallas_call x1, Pallas kernels, local(): pl.pallas_call(functools.partial(kernel, tms, chans), out_shape=pltpu.VME...  99.3 us

profile of v1, /device:TPU:13, one launch (start us, length us, event | category | flops | bytes accessed | tf_op | source)
XLA Modules:
  0.0 101.3 jit_solution(15779284758320941440)
XLA Ops:
  0.0 99.3 %shard_map.46 = bf16[2,2,32,16384]{3,2,1,0:T(8,128)(2,1)S(1)} custom-call(bf16[2,512,2048]{2,1,0:T(8,128)(2,1)} %samples.1, f32[8,2048]{1,0:T(8,128)} %taps_in.1, f32[4,2,8,2048]{3,2,1,0:T(8,128)} %constant.4.clone.coarse_in, f32[2,32,2048]{2,1,0:T(8,128)} %constant.5.clone.fine_in), custom_call_target="tpu_custom_call" | custom-call | tf_op jit(solution)/shard_map/pallas_call | solution.py:229
  99.3 2.0 %copy.6 = bf16[2,2,32,16384]{3,2,1,0:T(8,128)(2,1)} copy(bf16[2,2,32,16384]{3,2,1,0:T(8,128)(2,1)S(1)} %shard_map.46) | data formatting | bytes 8388608

commit v2 on v1

--- a/solution.py
+++ b/solution.py
@@ -15,7 +15,7 @@
 
 
 def base_tables(nfft, per_dev, count):
-    n = np.arange(nfft, dtype=np.int64)[None, :]
+    n = np.arange(nfft // 2, dtype=np.int64)[None, :]
 
     def pair(steps, scale):
         angle = (steps[:, None] * n % nfft) * (2.0 * np.pi / nfft)
@@ -28,8 +28,8 @@
 
 def kernel(
     tms, chans, samples, taps_in, coarse_in, fine_in, out,
-    xs, taps, coarse, fine, weighted, table, sp,
-    load_sem, base_sem, coarse_sem, halo_sem, own_sem, send_sem, recv_sem,
+    xs, taps, coarse, fine, stage, weighted, table, sp,
+    load_sem, base_sem, coarse_sem, halo_sem, own_sem, send_sem, recv_sem, met_sem,
 ):
     pols, frames, nfft = samples.shape
     tap_count = taps_in.shape[0]
@@ -68,12 +68,21 @@
 
     barrier = pltpu.get_barrier_semaphore()
 
-    for step in range(chans):
-        for turn_by in range(tms):
-            z, tm = group_of(step), lax.rem(my_tm + turn_by, tms)
-
-            if (step, turn_by) != (chans // 2, 0):
-                pl.semaphore_signal(barrier, inc=1, device_id=(tm, z), device_id_type=MESH)
+    facing, beside = group_of(0), lax.bitwise_xor(my_z, 1)
+    before = lax.rem(me + count - 1, count)
+
+    def signal(sem, tm, z):
+        pl.semaphore_signal(sem, inc=1, device_id=(tm, z), device_id_type=MESH)
+
+    signal(barrier, before // chans, lax.rem(before, chans))
+    signal(barrier, my_tm, beside)
+    for turn_by in range(tms):
+        signal(barrier, lax.rem(my_tm + turn_by, tms), facing)
+
+    def enter():
+        pl.semaphore_wait(barrier, tms + 2)
+        signal(met_sem.at[0], my_tm, beside)
+        halo.start()
 
     for step in range(1, chans):
         coarse_load(step).start()
@@ -93,30 +102,37 @@
     def filter_chunk(p, low, size):
         blocks = size // ROWS
         lane_blocks = nfft // LANES
+        slots = stage.shape[0]
 
         def body(step, _):
-            row = pl.multiple_of((step // lane_blocks) * ROWS, ROWS)
-            lane = pl.multiple_of(lax.rem(step, lane_blocks) * LANES, LANES)
-            x = xs[p, pl.ds(low + row, ROWS + HALO), pl.ds(lane, LANES)]
-            x = x.astype(jnp.float32)
-            w = taps[:, pl.ds(lane, LANES)]
-            total = None
-            for tap in range(tap_count):
-                by = tap_count - 1 - tap
-                moved = x if by == 0 else pltpu.roll(x, by, 0)
-                term = w[tap : tap + 1, :] * moved[HALO:, :]
-                total = term if total is None else total + term
-            weighted[pl.ds(row, ROWS), pl.ds(lane, LANES)] = total.astype(jnp.bfloat16)
+            for slot in range(slots):
+                at = step * slots + slot
+                row = pl.multiple_of((at // lane_blocks) * ROWS, ROWS)
+                lane = pl.multiple_of(lax.rem(at, lane_blocks) * LANES, LANES)
+                x = xs[p, pl.ds(low + row, ROWS + HALO), pl.ds(lane, LANES)]
+                stage[slot] = x.astype(jnp.float32)
+                w = taps[:, pl.ds(lane, LANES)]
+                total = None
+                for tap in range(tap_count):
+                    moved = stage[slot, pl.ds(HALO - tap_count + 1 + tap, ROWS), :]
+                    term = w[tap : tap + 1, :] * moved
+                    total = term if total is None else total + term
+                weighted[pl.ds(row, ROWS), pl.ds(lane, LANES)] = total.astype(jnp.bfloat16)
             return 0
 
-        lax.fori_loop(0, blocks * lane_blocks, body, 0)
+        lax.fori_loop(0, blocks * lane_blocks // slots, body, 0)
 
     def make_group(z):
         def body(tm, _):
             cos_i, sin_i = coarse[z, 0, pl.ds(tm, 1), :], coarse[z, 1, pl.ds(tm, 1), :]
             cos_j, sin_j = fine[0], fine[1]
-            table[z, tm, 0] = (cos_i * cos_j - sin_i * sin_j).astype(jnp.bfloat16)
-            table[z, tm, 1] = (-(sin_i * cos_j + cos_i * sin_j)).astype(jnp.bfloat16)
+            channel = (tm * chans + z) * per_dev + lax.broadcasted_iota(jnp.int32, (per_dev, 1), 0)
+            sign = (1 - 2 * lax.rem(channel, 2)).astype(jnp.float32)
+            for part, values in enumerate(
+                (cos_i * cos_j - sin_i * sin_j, -(sin_i * cos_j + cos_i * sin_j))
+            ):
+                table[z, tm, part, :, 0 : nfft // 2] = values.astype(jnp.bfloat16)
+                table[z, tm, part, :, nfft // 2 : nfft] = (values * sign).astype(jnp.bfloat16)
             return 0
 
         lax.fori_loop(0, tms, body, 0)
@@ -124,6 +140,11 @@
     fine_load.wait()
     coarse_load(0).wait()
     make_group(group_of(jnp.int32(0)))
+
+    @pl.when(my_z > chans // 2)
+    def _():
+        enter()
+
 
     def chunk(p, low, size, first):
         def group(step, _):
@@ -135,6 +156,20 @@
             )
             product = product.reshape(tms, 2, per_dev, size)
             sp[z, :, :, p, :, low : low + size] = product.astype(jnp.bfloat16)
+            if first:
+                @pl.when(jnp.logical_and(step == 0, my_z < chans // 2))
+                def _():
+                    enter()
+
+                @pl.when(step == 1)
+                def _():
+                    pl.semaphore_wait(met_sem.at[0], 1)
+                    signal(met_sem.at[1], my_tm, facing)
+
+                @pl.when(step == chans // 2)
+                def _():
+                    pl.semaphore_wait(met_sem.at[1], 1)
+
             def send(turn_by, _):
                 tm = lax.rem(my_tm + turn_by, tms)
                 dest = tm * chans + z
@@ -163,8 +198,10 @@
 
         filter_chunk(p, low, size)
         if first:
-            pl.semaphore_wait(barrier, count - 1)
-            halo.start()
+            @pl.when(my_z == chans // 2)
+            def _():
+                enter()
+
         lax.fori_loop(0, chans, group, 0)
 
     taps_load.wait()
@@ -223,7 +260,7 @@
     count = tms * chans
     per_dev = nfft // 2 // count
     coarse, fine = base_tables(nfft, per_dev, count)
-    coarse = coarse.reshape(2, tms, chans, nfft).transpose(2, 0, 1, 3)
+    coarse = coarse.reshape(2, tms, chans, nfft // 2).transpose(2, 0, 1, 3)
     vmem = pl.BlockSpec(memory_space=pltpu.VMEM)
     hbm = pl.BlockSpec(memory_space=pl.ANY)
     return pl.pallas_call(
@@ -234,8 +271,9 @@
         scratch_shapes=[
             pltpu.VMEM((pols, HALO + frames, nfft), jnp.bfloat16),
             pltpu.VMEM((tap_count, nfft), jnp.float32),
-            pltpu.VMEM((chans, 2, tms, nfft), jnp.float32),
-            pltpu.VMEM((2, per_dev, nfft), jnp.float32),
+            pltpu.VMEM((chans, 2, tms, nfft // 2), jnp.float32),
+            pltpu.VMEM((2, per_dev, nfft // 2), jnp.float32),
+            pltpu.VMEM((2, HALO + ROWS, LANES), jnp.float32),
             pltpu.VMEM((frames // 2, nfft), jnp.bfloat16),
             pltpu.VMEM((chans, tms, 2, per_dev, nfft), jnp.bfloat16),
             pltpu.VMEM((chans, tms, 2, pols, per_dev, frames), jnp.bfloat16),
@@ -246,6 +284,7 @@
             pltpu.SemaphoreType.DMA,
             pltpu.SemaphoreType.DMA((count,)),
             pltpu.SemaphoreType.DMA((count,)),
+            pltpu.SemaphoreType.REGULAR((2,)),
         ],
         compiler_params=pltpu.CompilerParams(
             collective_id=0, has_side_effects=True, vmem_limit_bytes=56 * 1024 * 1024

time: 101 us -> 101 us (level); the launches traced: 101 us -> 100 us
  Pallas kernels: 99.3 us -> 98.1 us
    pallas_call x1, Pallas kernels: 99.3 us -> 98.1 us  [local(): pl.pallas_call(functools.partial(kernel, tms, chans), out_shape=pltpu.VME...]
where the time goes in v2:
time: 101 us; the launch traced here: 100 us
  Pallas kernels  98.1 us (97%)
  local copies, waits for them, and re-layouts  2.02 us (2%)
    pallas_call x1, Pallas kernels, local(): pl.pallas_call(functools.partial(kernel, tms, chans), out_shape=pltpu.VME...  98.1 us

profile of v2, /device:TPU:13, one launch (start us, length us, event | category | flops | bytes accessed | tf_op | source)
XLA Modules:
  0.0 100.1 jit_solution(1340718126336734002)
XLA Ops:
  0.0 98.1 %shard_map.46 = bf16[2,2,32,16384]{3,2,1,0:T(8,128)(2,1)S(1)} custom-call(bf16[2,512,2048]{2,1,0:T(8,128)(2,1)} %samples.1, f32[8,2048]{1,0:T(8,128)} %taps_in.1, f32[4,2,8,1024]{3,2,1,0:T(8,128)} %constant.4.clone.coarse_in, f32[2,32,1024]{2,1,0:T(8,128)} %constant.5.clone.fine_in), custom_call_target="tpu_custom_call" | custom-call | tf_op jit(solution)/shard_map/pallas_call | solution.py:266
  98.1 2.0 %copy.6 = bf16[2,2,32,16384]{3,2,1,0:T(8,128)(2,1)} copy(bf16[2,2,32,16384]{3,2,1,0:T(8,128)(2,1)S(1)} %shard_map.46) | data formatting | bytes 8388608

commit v3 on v2

--- a/solution.py
+++ b/solution.py
@@ -43,8 +43,14 @@
     def group_of(step):
         return lax.bitwise_xor(my_z, lax.bitwise_xor(step, chans // 2))
 
+    near = jnp.where(my_z < chans // 2, chans // 2, chans // 2 - 1)
+
+    def first_group_of(step):
+        crossing = step < chans // 2
+        return lax.bitwise_xor(jnp.where(crossing, near, my_z), lax.rem(step, chans // 2))
+
     def coarse_load(step):
-        z = group_of(step)
+        z = first_group_of(step)
         return pltpu.make_async_copy(coarse_in.at[z], coarse.at[z], coarse_sem.at[step])
 
     taps_load = pltpu.make_async_copy(taps_in, taps, base_sem.at[0])
@@ -68,7 +74,8 @@
 
     barrier = pltpu.get_barrier_semaphore()
 
-    facing, beside = group_of(0), lax.bitwise_xor(my_z, 1)
+    beside = lax.bitwise_xor(my_z, 1)
+    inner = jnp.logical_or(my_z == chans // 2 - 1, my_z == chans // 2)
     before = lax.rem(me + count - 1, count)
 
     def signal(sem, tm, z):
@@ -76,18 +83,31 @@
 
     signal(barrier, before // chans, lax.rem(before, chans))
     signal(barrier, my_tm, beside)
-    for turn_by in range(tms):
-        signal(barrier, lax.rem(my_tm + turn_by, tms), facing)
+
+    @pl.when(inner)
+    def _():
+        for other in range(chans // 2):
+            for turn_by in range(tms):
+                signal(barrier, lax.rem(my_tm + turn_by, tms), lax.bitwise_xor(near, other))
 
     def enter():
         pl.semaphore_wait(barrier, tms + 2)
-        signal(met_sem.at[0], my_tm, beside)
         halo.start()
 
-    for step in range(1, chans):
-        coarse_load(step).start()
-    for load in loads[1:]:
-        load.start()
+        @pl.when(inner)
+        def _():
+            for turn_by in range(tms):
+                signal(met_sem.at[0], lax.rem(my_tm + turn_by, tms), near)
+
+    def meet(at, waits):
+        @pl.when(inner)
+        def _():
+            pl.semaphore_wait(met_sem.at[at], waits)
+            signal(met_sem.at[at], my_tm, beside)
+
+        @pl.when(jnp.logical_not(inner))
+        def _():
+            pl.semaphore_wait(met_sem.at[at], 1)
 
     after = lax.rem(me + 1, count)
     halo = pltpu.make_async_remote_copy(
@@ -122,8 +142,14 @@
 
         lax.fori_loop(0, blocks * lane_blocks // slots, body, 0)
 
-    def make_group(z):
-        def body(tm, _):
+    base = my_tm
+
+    def turned(turn_by):
+        return lax.rem(base + turn_by, tms)
+
+    def make_tables(z, start, width):
+        def body(turn_by, _):
+            tm = turned(turn_by)
             cos_i, sin_i = coarse[z, 0, pl.ds(tm, 1), :], coarse[z, 1, pl.ds(tm, 1), :]
             cos_j, sin_j = fine[0], fine[1]
             channel = (tm * chans + z) * per_dev + lax.broadcasted_iota(jnp.int32, (per_dev, 1), 0)
@@ -131,87 +157,115 @@
             for part, values in enumerate(
                 (cos_i * cos_j - sin_i * sin_j, -(sin_i * cos_j + cos_i * sin_j))
             ):
-                table[z, tm, part, :, 0 : nfft // 2] = values.astype(jnp.bfloat16)
-                table[z, tm, part, :, nfft // 2 : nfft] = (values * sign).astype(jnp.bfloat16)
-            return 0
-
-        lax.fori_loop(0, tms, body, 0)
-
-    fine_load.wait()
-    coarse_load(0).wait()
-    make_group(group_of(jnp.int32(0)))
-
-    @pl.when(my_z > chans // 2)
-    def _():
-        enter()
-
-
-    def chunk(p, low, size, first):
+                table[z, turn_by, part, :, 0 : nfft // 2] = values.astype(jnp.bfloat16)
+                table[z, turn_by, part, :, nfft // 2 : nfft] = (values * sign).astype(jnp.bfloat16)
+            return 0
+
+        lax.fori_loop(start, start + width, body, 0)
+
+    def transform(p, low, size, z, start, width):
+        rows = table[z, start : start + width].reshape(width * 2 * per_dev, nfft)
+        product = lax.dot_general(
+            rows, weighted[pl.ds(0, size), :], (((1,), (1,)), ((), ())),
+            preferred_element_type=jnp.float32,
+        )
+        product = product.reshape(width, 2, per_dev, size)
+        sp[z, start : start + width, :, p, :, low : low + size] = product.astype(jnp.bfloat16)
+
+    def send(p, low, size, z, start, width):
+        def body(turn_by, _):
+            tm = turned(turn_by)
+            dest = tm * chans + z
+
+            @pl.when(dest != me)
+            def _():
+                pltpu.make_async_remote_copy(
+                    src_ref=sp.at[z, turn_by, :, p, :, pl.ds(low, size)],
+                    dst_ref=out.at[:, p, :, pl.ds(pl.multiple_of(me * frames + low, LANES), size)],
+                    send_sem=send_sem.at[dest],
+                    recv_sem=recv_sem.at[me],
+                    device_id=(tm, z),
+                    device_id_type=MESH,
+                ).start()
+
+            return 0
+
+        lax.fori_loop(start, start + width, body, 0)
+
+    def first_chunk(p, low, size):
+        fine_load.wait()
+        coarse_load(0).wait()
+        for step in range(1, chans):
+            coarse_load(step).start()
+        for load in loads[1:]:
+            load.start()
+        make_tables(near, 0, lead)
+
+        @pl.when(my_z > chans // 2)
+        def _():
+            enter()
+
+        taps_load.wait()
+        loads[0].wait()
+        filter_chunk(p, low, size)
+
+        @pl.when(inner)
+        def _():
+            enter()
+
+        transform(p, low, size, near, 0, lead)
+
+        @pl.when(my_z < chans // 2 - 1)
+        def _():
+            enter()
+
+        send(p, low, size, near, 0, lead)
+        if lead < tms:
+            make_tables(near, lead, tms - lead)
+            transform(p, low, size, near, lead, tms - lead)
+            send(p, low, size, near, lead, tms - lead)
+
+        def group(step, _):
+            z = first_group_of(step)
+            coarse_load(step).wait()
+            make_tables(z, 0, tms)
+            transform(p, low, size, z, 0, tms)
+
+            @pl.when(step == 1)
+            def _():
+                meet(0, tms)
+
+                @pl.when(inner)
+                def _():
+                    for turn_by in range(1, tms):
+                        signal(met_sem.at[1], lax.rem(my_tm + turn_by, tms), my_z)
+
+            @pl.when(step == chans // 2)
+            def _():
+                meet(1, tms - 1)
+
+            send(p, low, size, z, 0, tms)
+            return 0
+
+        lax.fori_loop(1, chans, group, 0)
+
+    def chunk(p, low, size):
         def group(step, _):
             z = group_of(step)
-            rows = table[z].reshape(tms * 2 * per_dev, nfft)
-            product = lax.dot_general(
-                rows, weighted[pl.ds(0, size), :], (((1,), (1,)), ((), ())),
-                preferred_element_type=jnp.float32,
-            )
-            product = product.reshape(tms, 2, per_dev, size)
-            sp[z, :, :, p, :, low : low + size] = product.astype(jnp.bfloat16)
-            if first:
-                @pl.when(jnp.logical_and(step == 0, my_z < chans // 2))
-                def _():
-                    enter()
-
-                @pl.when(step == 1)
-                def _():
-                    pl.semaphore_wait(met_sem.at[0], 1)
-                    signal(met_sem.at[1], my_tm, facing)
-
-                @pl.when(step == chans // 2)
-                def _():
-                    pl.semaphore_wait(met_sem.at[1], 1)
-
-            def send(turn_by, _):
-                tm = lax.rem(my_tm + turn_by, tms)
-                dest = tm * chans + z
-
-                @pl.when(dest != me)
-                def _():
-                    pltpu.make_async_remote_copy(
-                        src_ref=sp.at[z, tm, :, p, :, pl.ds(low, size)],
-                        dst_ref=out.at[:, p, :, pl.ds(pl.multiple_of(me * frames + low, LANES), size)],
-                        send_sem=send_sem.at[dest],
-                        recv_sem=recv_sem.at[me],
-                        device_id=(tm, z),
-                        device_id_type=MESH,
-                    ).start()
-
-                return 0
-
-            lax.fori_loop(0, tms, send, 0)
-            if first:
-                @pl.when(step < chans - 1)
-                def _():
-                    coarse_load(step + 1).wait()
-                    make_group(group_of(step + 1))
-
+            transform(p, low, size, z, 0, tms)
+            send(p, low, size, z, 0, tms)
             return 0
 
         filter_chunk(p, low, size)
-        if first:
-            @pl.when(my_z == chans // 2)
-            def _():
-                enter()
-
         lax.fori_loop(0, chans, group, 0)
 
-    taps_load.wait()
-    loads[0].wait()
-    chunk(0, frames - quarter, quarter, True)
+    lead = max(tms // 4, 1)
+    first_chunk(0, frames - quarter, quarter)
     loads[1].wait()
-    chunk(0, half, quarter, False)
+    chunk(0, half, quarter)
     for p in range(1, pols):
         loads[1 + p].wait()
-        chunk(p, half, half, False)
+        chunk(p, half, half)
     halo.wait()
 
     @pl.when(me == 0)
@@ -220,34 +274,36 @@
 
     for p in range(pols):
         loads[1 + pols + p].wait()
-        chunk(p, 0, half, False)
+        chunk(p, 0, half)
 
     own = pltpu.make_async_copy(
-        sp.at[my_z, my_tm],
+        sp.at[my_z, 0],
         out.at[:, :, :, pl.ds(pl.multiple_of(me * frames, frames), frames)],
         own_sem,
     )
     own.start()
 
-    def block(z, tm):
-        peer = tm * chans + z
-        return pltpu.make_async_remote_copy(
-            src_ref=sp.at[z, tm],
-            dst_ref=out.at[:, :, :, pl.ds(pl.multiple_of(peer * frames, frames), frames)],
-            send_sem=send_sem.at[peer],
-            recv_sem=recv_sem.at[peer],
-            device_id=(tm, z),
-            device_id_type=MESH,
-        )
-
     def finish_group(step):
         z = group_of(step)
 
         def body(turn_by, _):
-            block(z, lax.rem(my_tm + turn_by, tms)).wait()
-            return 0
-
-        lax.fori_loop(1 if step == chans // 2 else 0, tms, body, 0)
+            tm = turned(turn_by)
+            peer = tm * chans + z
+
+            @pl.when(peer != me)
+            def _():
+                pltpu.make_async_remote_copy(
+                    src_ref=sp.at[z, turn_by],
+                    dst_ref=out.at[:, :, :, pl.ds(pl.multiple_of(peer * frames, frames), frames)],
+                    send_sem=send_sem.at[peer],
+                    recv_sem=recv_sem.at[peer],
+                    device_id=(tm, z),
+                    device_id_type=MESH,
+                ).wait()
+
+            return 0
+
+        lax.fori_loop(0, tms, body, 0)
 
     own.wait()
     for step in reversed(range(chans)):

time: 101 us -> 100 us (0.990)
  no operation moved by 1% of the time
where the time goes in v3:
time: 100 us; the launch traced here: 99.9 us
  Pallas kernels  97.8 us (98%)
  local copies, waits for them, and re-layouts  2.02 us (2%)
    pallas_call x1, Pallas kernels, local(): pl.pallas_call(functools.partial(kernel, tms, chans), out_shape=pltpu.VME...  97.8 us
    unnamed x1, local copies, waits for them, and re-layouts  2.02 us

profile of v3, /device:TPU:13, one launch (start us, length us, event | category | flops | bytes accessed | tf_op | source)
XLA Modules:
  0.0 99.9 jit_solution(13795360217298141599)
XLA Ops:
  0.0 97.8 %shard_map.46 = bf16[2,2,32,16384]{3,2,1,0:T(8,128)(2,1)S(1)} custom-call(bf16[2,512,2048]{2,1,0:T(8,128)(2,1)} %samples.1, f32[8,2048]{1,0:T(8,128)} %taps_in.1, f32[4,2,8,1024]{3,2,1,0:T(8,128)} %constant.4.clone.coarse_in, f32[2,32,1024]{2,1,0:T(8,128)} %constant.5.clone.fine_in), custom_call_target="tpu_custom_call" | custom-call | tf_op jit(solution)/shard_map/pallas_call | solution.py:322
  97.8 2.0 %copy.6 = bf16[2,2,32,16384]{3,2,1,0:T(8,128)(2,1)} copy(bf16[2,2,32,16384]{3,2,1,0:T(8,128)(2,1)S(1)} %shard_map.46) | data formatting | bytes 8388608

commit v4 on v3

--- a/solution.py
+++ b/solution.py
@@ -58,7 +58,7 @@
     spans = [
         (0, frames - quarter - HALO, quarter + HALO),
         (0, half - HALO, quarter),
-        *((p, half - HALO, half + HALO) for p in range(1, pols)),
+        *((p, half - HALO, half) for p in range(1, pols)),
         *((p, 0, half - HALO) for p in range(pols)),
     ]
     loads = [
@@ -67,10 +67,16 @@
         )
         for at, (p, low, size) in enumerate(spans)
     ]
+    tail_load = pltpu.make_async_copy(
+        samples.at[1:pols, pl.ds(frames - HALO, HALO)],
+        xs.at[1:pols, pl.ds(frames, HALO)],
+        base_sem.at[2],
+    )
     fine_load.start()
     coarse_load(0).start()
     taps_load.start()
     loads[0].start()
+    tail_load.start()
 
     barrier = pltpu.get_barrier_semaphore()
 
@@ -111,7 +117,7 @@
 
     after = lax.rem(me + 1, count)
     halo = pltpu.make_async_remote_copy(
-        src_ref=samples.at[:, pl.ds(frames - HALO, HALO), :],
+        src_ref=xs.at[:, pl.ds(frames, HALO), :],
         dst_ref=xs.at[:, pl.ds(0, HALO), :],
         send_sem=halo_sem.at[0],
         recv_sem=halo_sem.at[1],
@@ -172,8 +178,14 @@
         product = product.reshape(width, 2, per_dev, size)
         sp[z, start : start + width, :, p, :, low : low + size] = product.astype(jnp.bfloat16)
 
-    def send(p, low, size, z, start, width):
-        def body(turn_by, _):
+    def send(p, low, size, z, start, width, halves=False):
+        def body(step, _):
+            turn_by = step
+            if halves:
+                part = tms // 2
+                tm = step // part * part + lax.rem(my_tm + step, part)
+                turn_by = lax.rem(tm - my_tm + tms, tms)
+
             tm = turned(turn_by)
             dest = tm * chans + z
 
@@ -199,14 +211,15 @@
             coarse_load(step).start()
         for load in loads[1:]:
             load.start()
+        taps_load.wait()
+        tail_load.wait()
+        loads[0].wait()
+
+        @pl.when(my_z > chans // 2)
+        def _():
+            enter()
+
         make_tables(near, 0, lead)
-
-        @pl.when(my_z > chans // 2)
-        def _():
-            enter()
-
-        taps_load.wait()
-        loads[0].wait()
         filter_chunk(p, low, size)
 
         @pl.when(inner)
@@ -253,7 +266,7 @@
         def group(step, _):
             z = group_of(step)
             transform(p, low, size, z, 0, tms)
-            send(p, low, size, z, 0, tms)
+            send(p, low, size, z, 0, tms, p == pols - 1 and low == 0)
             return 0
 
         filter_chunk(p, low, size)
@@ -306,7 +319,7 @@
         lax.fori_loop(0, tms, body, 0)
 
     own.wait()
-    for step in reversed(range(chans)):
+    for step in [*range(2, chans), 0, 1]:
         finish_group(step)
 
 
@@ -334,7 +347,7 @@
             pltpu.VMEM((chans, tms, 2, per_dev, nfft), jnp.bfloat16),
             pltpu.VMEM((chans, tms, 2, pols, per_dev, frames), jnp.bfloat16),
             pltpu.SemaphoreType.DMA((2 * pols + 1,)),
-            pltpu.SemaphoreType.DMA((2,)),
+            pltpu.SemaphoreType.DMA((3,)),
             pltpu.SemaphoreType.DMA((chans,)),
             pltpu.SemaphoreType.DMA((2,)),
             pltpu.SemaphoreType.DMA,

time: 100 us -> 100 us (level)
  no operation moved by 1% of the time
where the time goes in v4:
time: 100 us
  Pallas kernels  97.9 us (98%)
  local copies, waits for them, and re-layouts  2.02 us (2%)
    pallas_call x1, Pallas kernels, local(): pl.pallas_call(functools.partial(kernel, tms, chans), out_shape=pltpu.VME...  97.9 us
    unnamed x1, local copies, waits for them, and re-layouts  2.02 us

profile of v4, /device:TPU:13, one launch (start us, length us, event | category | flops | bytes accessed | tf_op | source)
XLA Modules:
  0.0 100.0 jit_solution(16478320257061117228)
XLA Ops:
  0.0 97.9 %shard_map.46 = bf16[2,2,32,16384]{3,2,1,0:T(8,128)(2,1)S(1)} custom-call(bf16[2,512,2048]{2,1,0:T(8,128)(2,1)} %samples.1, f32[8,2048]{1,0:T(8,128)} %taps_in.1, f32[4,2,8,1024]{3,2,1,0:T(8,128)} %constant.4.clone.coarse_in, f32[2,32,1024]{2,1,0:T(8,128)} %constant.5.clone.fine_in), custom_call_target="tpu_custom_call" | custom-call | tf_op jit(solution)/shard_map/pallas_call | solution.py:335
  97.9 2.0 %copy.6 = bf16[2,2,32,16384]{3,2,1,0:T(8,128)(2,1)} copy(bf16[2,2,32,16384]{3,2,1,0:T(8,128)(2,1)S(1)} %shard_map.46) | data formatting | bytes 8388608

commit v5 on v4

--- a/solution.py
+++ b/solution.py
@@ -266,7 +266,7 @@
         def group(step, _):
             z = group_of(step)
             transform(p, low, size, z, 0, tms)
-            send(p, low, size, z, 0, tms, p == pols - 1 and low == 0)
+            send(p, low, size, z, 0, tms, True)
             return 0
 
         filter_chunk(p, low, size)

time: 100 us -> 100 us (level)
  no operation moved by 1% of the time
where the time goes in v5:
time: 100 us
  Pallas kernels  97.9 us (98%)
  local copies, waits for them, and re-layouts  2.02 us (2%)
    pallas_call x1, Pallas kernels, local(): pl.pallas_call(functools.partial(kernel, tms, chans), out_shape=pltpu.VME...  97.9 us
    unnamed x1, local copies, waits for them, and re-layouts  2.02 us

profile of v5, /device:TPU:13, one launch (start us, length us, event | category | flops | bytes accessed | tf_op | source)
XLA Modules:
  0.0 100.0 jit_solution(15554819342139027115)
XLA Ops:
  0.0 97.9 %shard_map.46 = bf16[2,2,32,16384]{3,2,1,0:T(8,128)(2,1)S(1)} custom-call(bf16[2,512,2048]{2,1,0:T(8,128)(2,1)} %samples.1, f32[8,2048]{1,0:T(8,128)} %taps_in.1, f32[4,2,8,1024]{3,2,1,0:T(8,128)} %constant.4.clone.coarse_in, f32[2,32,1024]{2,1,0:T(8,128)} %constant.5.clone.fine_in), custom_call_target="tpu_custom_call" | custom-call | tf_op jit(solution)/shard_map/pallas_call | solution.py:335
  97.9 2.0 %copy.6 = bf16[2,2,32,16384]{3,2,1,0:T(8,128)(2,1)} copy(bf16[2,2,32,16384]{3,2,1,0:T(8,128)(2,1)S(1)} %shard_map.46) | data formatting | bytes 8388608
